TPU v7x, 256 devices: a 4x2x16 block of a 4x16x16 slice. The times are simulated.
256 devices in a mesh: groups: 2 (over y), seq: 16 (over z), section: 4 (over x), mp: 2 (over core).
Axes of the slice: x: 4, y: 2, z: 16, core: 2. Of those that a mesh axis runs over, the one named last changes fastest.
The devices are a block of a 4x16x16 slice.
Arguments:
- light_queries: bfloat16 [8192, 8192], P(('groups', 'seq'), ('section', 'mp')), parts along dimension 0, may hold values from -6 to 6
- light_keys: bfloat16 [8192, 8192], P(('groups', 'seq'), ('section', 'mp')), parts along dimension 0, may hold values from -6 to 6
- light_values: bfloat16 [8192, 8192], P(('groups', 'seq'), ('section', 'mp')), parts along dimension 0, may hold values from -6 to 6
- decay_log: float32 [8192, 64], P(('groups', 'seq'), ('section', 'mp')), parts along dimension 0, may hold values from -1 to 0
- norm_gain: float32 [8192], P(('section', 'mp')), may hold values from 0.25 to 1.75
- soft_queries: bfloat16 [8192, 8192], P(('groups', 'seq'), ('section', 'mp')), parts along dimension 0, may hold values from -150 to 150
- soft_keys: bfloat16 [8192, 1024], P(('groups', 'seq'), ('section', 'mp')), parts along dimension 0, may hold values from -6 to 6
- soft_values: bfloat16 [8192, 1024], P(('groups', 'seq'), ('section', 'mp')), parts along dimension 0, may hold values from -6 to 6
- lengths: int32 [32], P('groups'), parts along dimension 0, may hold values from 1 to 256, 3072 in all
Outputs:
- light_out: bfloat16 [8192, 8192], P(('groups', 'seq'), ('section', 'mp')), parts along dimension 0
- soft_out: bfloat16 [8192, 8192], P(('groups', 'seq'), ('section', 'mp')), parts along dimension 0
There are 2 independent parts, one for each index of `groups`. A program takes and returns all parts, laid end to end along the dimension named above; an argument that names none is the same for every part. Nothing has to cross between parts.
Inputs may be any that keep to these rules, and one draw needn't show every extreme that they name: The live tokens of a block stand at its first slots; the lengths sum to 3072.
All inputs are finite; a program needn't handle non-finite values.
Results may differ from a plain program's by a relative error of at most 0.007.
Values may be sent and summed in bfloat16 or wider, within the bound.
A program may use at most 64 MiB of HBM per device.

v0:
```python
from functools import partial

import jax
import jax.numpy as jnp
from jax import lax
from jax.sharding import PartitionSpec as P


def sent_to_all(x, axis):
    length = lax.axis_size(axis)
    return lax.all_to_all(jnp.broadcast_to(x[None], (length, *x.shape)), axis, 0, 0, tiled=True)


def in_order(parts, dim):
    dims = list(parts.shape[1:])
    dims[dim] *= parts.shape[0]
    return jnp.moveaxis(parts, 0, dim).reshape(dims)


def gathered_copies(x, axis, dim):
    parts = sent_to_all(x, axis)
    return in_order(parts, dim)


def side_by_side(arrays, axis, dim, along):
    ends, at = ([], 0)
    for a in arrays[:-1]:
        at += a.shape[along]
        ends.append(at)
    both = jnp.concatenate(arrays, axis=along)
    return tuple(jnp.split(lax.all_gather(both, axis, axis=dim, tiled=True), ends, axis=along))


def live_slots(lengths, device, row_count):
    owners = jnp.arange(lengths.shape[0], dtype=jnp.int32)
    own_length = jnp.sum(jnp.where(owners == device, lengths, 0))
    return jnp.arange(row_count, dtype=jnp.int32) < own_length


def keep_state(fold_state):
    return fold_state


def attend_keys(fold_state, query_block, query_start, key_block, value_block, key_start, key_live):
    row_count = query_block.shape[0]
    head_width = query_block.shape[-1]
    scores = jnp.einsum(
        "tkgd,skd->kgts", query_block, key_block, preferred_element_type=jnp.float32
    ) * head_width ** (-0.5)
    query_pos = query_start + jnp.arange(row_count, dtype=jnp.int32)
    key_pos = key_start + jnp.arange(key_block.shape[0], dtype=jnp.int32)
    allowed = (key_pos[None, :] <= query_pos[:, None]) & key_live[None, :]
    scores = jnp.where(allowed, scores, -jnp.inf)
    peak_old, total_old, running_sum = fold_state
    peak_new = jnp.maximum(peak_old, jnp.max(scores, axis=-1))
    anchor = jnp.where(peak_new == -jnp.inf, 0.0, peak_new)
    weights_now = jnp.exp(scores - anchor[..., None])
    shrink = jnp.exp(peak_old - anchor)
    total_new = shrink * total_old + jnp.sum(weights_now, axis=-1)
    running_sum = shrink[..., None] * running_sum + jnp.einsum(
        "kgts,skd->kgtd",
        weights_now.astype(jnp.bfloat16),
        value_block,
        preferred_element_type=jnp.float32,
    )
    return (peak_new, total_new, running_sum)


def body(
    light_queries,
    light_keys,
    light_values,
    decay_log,
    norm_gain,
    soft_queries,
    soft_keys,
    soft_values,
    lengths,
):
    tok_rows = light_queries.shape[0]
    head_count = decay_log.shape[1]
    head_width = light_queries.shape[1] // head_count
    device = lax.axis_index("seq")
    seq_count = lax.axis_size("seq")
    live_rows = live_slots(lengths, device, tok_rows)
    score_scale = head_width ** (-0.5)
    query_heads = light_queries.reshape(tok_rows, head_count, head_width)
    key_heads = light_keys.reshape(tok_rows, head_count, head_width)
    value_heads = light_values.reshape(tok_rows, head_count, head_width)
    masked = jnp.where(live_rows[:, None], decay_log, 0.0)
    running = jnp.cumsum(masked, axis=0)
    ending = running[-1]
    scores = jnp.einsum("thd,shd->hts", query_heads, key_heads, preferred_element_type=jnp.float32)
    token_slot_index = jnp.arange(tok_rows, dtype=jnp.int32)
    causal = token_slot_index[:, None] >= token_slot_index[None, :]
    log_gaps = running.T[:, :, None] - running.T[:, None, :]
    allowed = causal[None] & live_rows[None, None, :]
    weights = jnp.where(allowed, jnp.exp(jnp.where(causal[None], log_gaps, 0.0)), 0.0)
    intra_weight = (scores * score_scale * weights).astype(jnp.bfloat16)
    inside = jnp.einsum(
        "hts,shd->thd", intra_weight, value_heads, preferred_element_type=jnp.float32
    )
    fading = jnp.exp(ending[None, :] - running) * live_rows[:, None]
    block_keys = (key_heads.astype(jnp.float32) * fading[:, :, None]).astype(jnp.bfloat16)
    block_state = jnp.einsum(
        "thd,the->hde", block_keys, value_heads, preferred_element_type=jnp.float32
    )
    totals = gathered_copies(ending[None, :], "seq", 0)
    owners = jnp.arange(seq_count, dtype=jnp.int32)
    between = (owners[None, :] > owners[:, None]) & (owners[None, :] < device)
    fold_logs = jnp.sum(jnp.where(between[:, :, None], totals[None, :, :], 0.0), axis=1)
    shard_block = lax.all_gather(
        block_state[None].astype(jnp.bfloat16), "seq", axis=0, tiled=True
    ).astype(jnp.float32)
    sources = jnp.arange(shard_block.shape[0], dtype=jnp.int32)
    factors = jnp.where((sources < device)[:, None], jnp.exp(fold_logs), 0.0)
    entering = jnp.zeros_like(block_state) + jnp.einsum("nh,nhde->hde", factors, shard_block)
    across = (
        jnp.einsum("thd,hde->the", query_heads.astype(jnp.float32) * score_scale, entering)
        * jnp.exp(running)[:, :, None]
    )
    combined = inside + across
    normed = (
        combined
        * lax.rsqrt(jnp.mean(combined * combined, axis=-1, keepdims=True) + 1e-06)
        * norm_gain.reshape(head_count, head_width)
    )
    light_out = (
        jnp.where(live_rows[:, None, None], normed, 0.0)
        .astype(jnp.bfloat16)
        .reshape(tok_rows, head_count * head_width)
    )
    kv_count = soft_keys.shape[1] // head_width
    group_size = soft_queries.shape[1] // head_width // kv_count
    soft_heads = soft_queries.reshape(tok_rows, kv_count, group_size, head_width)
    query_sets = ((soft_heads, device * tok_rows),)

    def empty_state(query_block):
        row_count = query_block.shape[0]
        return (
            jnp.full((kv_count, group_size, row_count), -jnp.inf, jnp.float32),
            jnp.zeros((kv_count, group_size, row_count), jnp.float32),
            jnp.zeros((kv_count, group_size, row_count, head_width), jnp.float32),
        )

    initial = tuple((empty_state(query_block) for query_block, query_start in query_sets))
    states = initial
    key_shards, value_shards = side_by_side((soft_keys, soft_values), "seq", 0, 1)
    shard_count = key_shards.shape[0] // tok_rows
    key_stack = key_shards.reshape(shard_count, tok_rows, kv_count, head_width)
    value_stack = value_shards.reshape(shard_count, tok_rows, kv_count, head_width)

    def per_shard(current, inputs):
        key_block, value_block, offset = inputs
        key_start = offset * tok_rows
        key_live = live_slots(lengths, key_start // tok_rows, tok_rows)
        updated = []
        for (query_block, query_start), fold_state in zip(query_sets, current):
            query_last = query_start + query_block.shape[0] - 1
            attend_here = partial(
                attend_keys,
                query_block=query_block,
                query_start=query_start,
                key_block=key_block,
                value_block=value_block,
                key_start=key_start,
                key_live=key_live,
            )
            updated.append(lax.cond(key_start <= query_last, attend_here, keep_state, fold_state))
        return (tuple(updated), None)

    states, unused = lax.scan(
        per_shard, states, (key_stack, value_stack, jnp.arange(shard_count, dtype=jnp.int32))
    )
    peak_value, total_value, running_sum = states[0]
    result = running_sum / total_value[..., None]
    soft_rows = (
        result.transpose(2, 0, 1, 3)
        .reshape(result.shape[2], kv_count * group_size * head_width)
        .astype(jnp.bfloat16)
    )
    soft_out = jnp.where(live_rows[:, None], soft_rows, jnp.zeros_like(soft_rows))
    return (light_out, soft_out)


def solution(mesh):
    return jax.shard_map(
        body,
        mesh=mesh,
        in_specs=(
            P(("groups", "seq"), ("section", "mp")),
            P(("groups", "seq"), ("section", "mp")),
            P(("groups", "seq"), ("section", "mp")),
            P(("groups", "seq"), ("section", "mp")),
            P(("section", "mp")),
            P(("groups", "seq"), ("section", "mp")),
            P(("groups", "seq"), ("section", "mp")),
            P(("groups", "seq"), ("section", "mp")),
            P("groups"),
        ),
        out_specs=(
            P(("groups", "seq"), ("section", "mp")),
            P(("groups", "seq"), ("section", "mp")),
        ),
        check_vma=False,
    )
```

profile of v0, /device:TPU:1952, one launch (start us, length us, event | category | flops | bytes accessed | tf_op | source)
XLA Modules:
  0.0 181.1 jit_solution(13318923772529070674)
XLA Ops:
  7.3 1.6 pad_maximum_fusion
  10.3 1.3 fusion.40
  14.0 2.1 %convolution_convert_fusion = bf16[8,128,128]{2,1,0:T(8,128)(2,1)} fusion(bf16[256,8,128]{0,2,1:T(8,128)(2,1)S(1)} %bitcast.116, f32[256,8]{0,1:T(8,128)S(1)} %exponential_multiply_fusion, bf16[256,1024]{1,0:T(8,128)(2,1)} %param.15), kind=kOutput, calls=%fused_computation.33 | convolution fusion | flops 68026368 | bytes 1318912 | tf_op jit(solution)/shard_map/thd,the->hde/dot_general | solution.py:105
  16.8 4.5 %all-to-all-start = ((f32[16,1,8]{2,1,0:T(1,128)}), f32[16,1,8]{2,1,0:T(1,128)S(1)}, u32[]{:S(2)}, u32[]{:S(2)}) async-start(f32[16,1,8]{2,1,0:T(1,128)} %broadcast_in_dim.173), calls=%async_computation | async-start | bytes 16384 | tf_op jit(solution)/shard_map/all_to_all | solution.py:11
  21.5 2.1 %convolution_bitcast_fusion.2 = f32[256,8,128]{0,2,1:T(8,128)} fusion(bf16[256,8,128]{0,2,1:T(8,128)(2,1)S(1)} %bitcast.117, f32[8,256]{1,0:T(8,128)S(1)} %add_bitcast_fusion.1, pred[256,256]{1,0:T(8,128)(4,1)S(1)} %iota_compare_fusion, pred[256,256]{1,0:T(8,128)(4,1)S(1)} %broadcast_and_fusion, bf16[256,1024]{1,0:T(8,128)(2,1)S(1)} %copy-done.5, ...), kind=kOutput, calls=%fused_computation.32 | convolution fusion | flops 271581184 | bytes 2760704 | tf_op jit(solution)/shard_map/hts,shd->thd/dot_general | solution.py:100
  24.1 7.1 %all-to-all-done = f32[16,1,8]{2,1,0:T(1,128)S(1)} async-done(((f32[16,1,8]{2,1,0:T(1,128)}), f32[16,1,8]{2,1,0:T(1,128)S(1)}, u32[]{:S(2)}, u32[]{:S(2)}) %all-to-all-start) | async-done | bytes 544 | tf_op jit(solution)/shard_map/all_to_all | solution.py:11
  31.5 43.8 %all-gather.4.cloned.1.call-done = bf16[4096,256]{1,0:T(8,128)(2,1)} async-done(((bf16[256,256]{1,0:T(8,128)(2,1)}), bf16[4096,256]{1,0:T(8,128)(2,1)}) %all-gather.4.cloned.1.call-update) | async-done | bytes 2097168 | tf_op jit(solution)/shard_map/all_gather | solution.py:31
  75.3 2.7 %fusion.47 = (bf16[4096,128]{1,0:T(8,128)(2,1)S(1)}, bf16[4096,128]{1,0:T(8,128)(2,1)}) fusion(bf16[4096,256]{1,0:T(8,128)(2,1)} %all-gather.4.cloned.1.call-done), kind=kLoop, calls=%fused_computation.82 | loop fusion | bytes 4194304 | tf_op jit(solution)/shard_map/split | solution.py:31
  78.1 89.5 %while.17 = (s32[]{:T(128)}, f32[1,8,256]{2,1,0:T(8,128)S(1)}, f32[1,8,256]{2,1,0:T(8,128)S(1)}, f32[1,8,256,128]{3,2,1,0:T(8,128)S(1)}, s32[16]{0:T(128)S(1)}, ...) while((s32[]{:T(128)}, f32[1,8,256]{2,1,0:T(8,128)S(1)}, ...), condition=%wide.region_11.12_spmd, body=%wide.region_5.11_spmd.sunk | while | flops 272780096 | bytes 9330361 | solution.py:172
  79.5 4.2 %conditional.2 = ((f32[1,8,256]{2,1,0:T(8,128)S(1)}, f32[1,8,256]{2,1,0:T(8,128)S(1)}, f32[1,8,256,128]{3,2,1,0:T(8,128)S(1)})) conditional(s32[]{:T(128)} %convert_element_type.89, (f32[1,8,256]{2,1,0:T(8,128)S(1)}, f32[1,8,256]{2,1,0:T(8,128)S(1)}, f32[1,8,256,128]{3,2,1,0:T(8,128)S(1)}) %tuple.78, (s32[]{:T(128)}, s32[]{:T(128)}, s32[]{:T(128)}, ...), branch_computations={%region_6.6_spmd, %region_7.10_spmd.clone} | conditional | flops 272780096 | bytes 9328974 | solution.py:169
  85.1 4.2 %conditional.2 = ((f32[1,8,256]{2,1,0:T(8,128)S(1)}, f32[1,8,256]{2,1,0:T(8,128)S(1)}, f32[1,8,256,128]{3,2,1,0:T(8,128)S(1)})) conditional(s32[]{:T(128)} %convert_element_type.89, (f32[1,8,256]{2,1,0:T(8,128)S(1)}, f32[1,8,256]{2,1,0:T(8,128)S(1)}, f32[1,8,256,128]{3,2,1,0:T(8,128)S(1)}) %tuple.78, (s32[]{:T(128)}, s32[]{:T(128)}, s32[]{:T(128)}, ...), branch_computations={%region_6.6_spmd, %region_7.10_spmd.clone} | conditional | flops 272780096 | bytes 9328974 | solution.py:169
  90.7 4.2 %conditional.2 = ((f32[1,8,256]{2,1,0:T(8,128)S(1)}, f32[1,8,256]{2,1,0:T(8,128)S(1)}, f32[1,8,256,128]{3,2,1,0:T(8,128)S(1)})) conditional(s32[]{:T(128)} %convert_element_type.89, (f32[1,8,256]{2,1,0:T(8,128)S(1)}, f32[1,8,256]{2,1,0:T(8,128)S(1)}, f32[1,8,256,128]{3,2,1,0:T(8,128)S(1)}) %tuple.78, (s32[]{:T(128)}, s32[]{:T(128)}, s32[]{:T(128)}, ...), branch_computations={%region_6.6_spmd, %region_7.10_spmd.clone} | conditional | flops 272780096 | bytes 9328974 | solution.py:169
  92.2 1.3 fusion.46
  96.3 4.2 %conditional.2 = ((f32[1,8,256]{2,1,0:T(8,128)S(1)}, f32[1,8,256]{2,1,0:T(8,128)S(1)}, f32[1,8,256,128]{3,2,1,0:T(8,128)S(1)})) conditional(s32[]{:T(128)} %convert_element_type.89, (f32[1,8,256]{2,1,0:T(8,128)S(1)}, f32[1,8,256]{2,1,0:T(8,128)S(1)}, f32[1,8,256,128]{3,2,1,0:T(8,128)S(1)}) %tuple.78, (s32[]{:T(128)}, s32[]{:T(128)}, s32[]{:T(128)}, ...), branch_computations={%region_6.6_spmd, %region_7.10_spmd.clone} | conditional | flops 272780096 | bytes 9328974 | solution.py:169
  97.8 1.3 fusion.46
  101.9 4.2 %conditional.2 = ((f32[1,8,256]{2,1,0:T(8,128)S(1)}, f32[1,8,256]{2,1,0:T(8,128)S(1)}, f32[1,8,256,128]{3,2,1,0:T(8,128)S(1)})) conditional(s32[]{:T(128)} %convert_element_type.89, (f32[1,8,256]{2,1,0:T(8,128)S(1)}, f32[1,8,256]{2,1,0:T(8,128)S(1)}, f32[1,8,256,128]{3,2,1,0:T(8,128)S(1)}) %tuple.78, (s32[]{:T(128)}, s32[]{:T(128)}, s32[]{:T(128)}, ...), branch_computations={%region_6.6_spmd, %region_7.10_spmd.clone} | conditional | flops 272780096 | bytes 9328974 | solution.py:169
  107.5 4.2 %conditional.2 = ((f32[1,8,256]{2,1,0:T(8,128)S(1)}, f32[1,8,256]{2,1,0:T(8,128)S(1)}, f32[1,8,256,128]{3,2,1,0:T(8,128)S(1)})) conditional(s32[]{:T(128)} %convert_element_type.89, (f32[1,8,256]{2,1,0:T(8,128)S(1)}, f32[1,8,256]{2,1,0:T(8,128)S(1)}, f32[1,8,256,128]{3,2,1,0:T(8,128)S(1)}) %tuple.78, (s32[]{:T(128)}, s32[]{:T(128)}, s32[]{:T(128)}, ...), branch_computations={%region_6.6_spmd, %region_7.10_spmd.clone} | conditional | flops 272780096 | bytes 9328974 | solution.py:169
  113.0 4.2 %conditional.2 = ((f32[1,8,256]{2,1,0:T(8,128)S(1)}, f32[1,8,256]{2,1,0:T(8,128)S(1)}, f32[1,8,256,128]{3,2,1,0:T(8,128)S(1)})) conditional(s32[]{:T(128)} %convert_element_type.89, (f32[1,8,256]{2,1,0:T(8,128)S(1)}, f32[1,8,256]{2,1,0:T(8,128)S(1)}, f32[1,8,256,128]{3,2,1,0:T(8,128)S(1)}) %tuple.78, (s32[]{:T(128)}, s32[]{:T(128)}, s32[]{:T(128)}, ...), branch_computations={%region_6.6_spmd, %region_7.10_spmd.clone} | conditional | flops 272780096 | bytes 9328974 | solution.py:169
  118.6 4.2 %conditional.2 = ((f32[1,8,256]{2,1,0:T(8,128)S(1)}, f32[1,8,256]{2,1,0:T(8,128)S(1)}, f32[1,8,256,128]{3,2,1,0:T(8,128)S(1)})) conditional(s32[]{:T(128)} %convert_element_type.89, (f32[1,8,256]{2,1,0:T(8,128)S(1)}, f32[1,8,256]{2,1,0:T(8,128)S(1)}, f32[1,8,256,128]{3,2,1,0:T(8,128)S(1)}) %tuple.78, (s32[]{:T(128)}, s32[]{:T(128)}, s32[]{:T(128)}, ...), branch_computations={%region_6.6_spmd, %region_7.10_spmd.clone} | conditional | flops 272780096 | bytes 9328974 | solution.py:169
  120.1 1.3 fusion.46
  124.2 4.2 %conditional.2 = ((f32[1,8,256]{2,1,0:T(8,128)S(1)}, f32[1,8,256]{2,1,0:T(8,128)S(1)}, f32[1,8,256,128]{3,2,1,0:T(8,128)S(1)})) conditional(s32[]{:T(128)} %convert_element_type.89, (f32[1,8,256]{2,1,0:T(8,128)S(1)}, f32[1,8,256]{2,1,0:T(8,128)S(1)}, f32[1,8,256,128]{3,2,1,0:T(8,128)S(1)}) %tuple.78, (s32[]{:T(128)}, s32[]{:T(128)}, s32[]{:T(128)}, ...), branch_computations={%region_6.6_spmd, %region_7.10_spmd.clone} | conditional | flops 272780096 | bytes 9328974 | solution.py:169
  125.7 1.3 fusion.46
  129.8 4.2 %conditional.2 = ((f32[1,8,256]{2,1,0:T(8,128)S(1)}, f32[1,8,256]{2,1,0:T(8,128)S(1)}, f32[1,8,256,128]{3,2,1,0:T(8,128)S(1)})) conditional(s32[]{:T(128)} %convert_element_type.89, (f32[1,8,256]{2,1,0:T(8,128)S(1)}, f32[1,8,256]{2,1,0:T(8,128)S(1)}, f32[1,8,256,128]{3,2,1,0:T(8,128)S(1)}) %tuple.78, (s32[]{:T(128)}, s32[]{:T(128)}, s32[]{:T(128)}, ...), branch_computations={%region_6.6_spmd, %region_7.10_spmd.clone} | conditional | flops 272780096 | bytes 9328974 | solution.py:169
  135.4 4.2 %conditional.2 = ((f32[1,8,256]{2,1,0:T(8,128)S(1)}, f32[1,8,256]{2,1,0:T(8,128)S(1)}, f32[1,8,256,128]{3,2,1,0:T(8,128)S(1)})) conditional(s32[]{:T(128)} %convert_element_type.89, (f32[1,8,256]{2,1,0:T(8,128)S(1)}, f32[1,8,256]{2,1,0:T(8,128)S(1)}, f32[1,8,256,128]{3,2,1,0:T(8,128)S(1)}) %tuple.78, (s32[]{:T(128)}, s32[]{:T(128)}, s32[]{:T(128)}, ...), branch_computations={%region_6.6_spmd, %region_7.10_spmd.clone} | conditional | flops 272780096 | bytes 9328974 | solution.py:169
  136.9 1.3 fusion.46
  141.0 4.2 %conditional.2 = ((f32[1,8,256]{2,1,0:T(8,128)S(1)}, f32[1,8,256]{2,1,0:T(8,128)S(1)}, f32[1,8,256,128]{3,2,1,0:T(8,128)S(1)})) conditional(s32[]{:T(128)} %convert_element_type.89, (f32[1,8,256]{2,1,0:T(8,128)S(1)}, f32[1,8,256]{2,1,0:T(8,128)S(1)}, f32[1,8,256,128]{3,2,1,0:T(8,128)S(1)}) %tuple.78, (s32[]{:T(128)}, s32[]{:T(128)}, s32[]{:T(128)}, ...), branch_computations={%region_6.6_spmd, %region_7.10_spmd.clone} | conditional | flops 272780096 | bytes 9328974 | solution.py:169
  142.5 1.3 fusion.46
  146.6 4.2 %conditional.2 = ((f32[1,8,256]{2,1,0:T(8,128)S(1)}, f32[1,8,256]{2,1,0:T(8,128)S(1)}, f32[1,8,256,128]{3,2,1,0:T(8,128)S(1)})) conditional(s32[]{:T(128)} %convert_element_type.89, (f32[1,8,256]{2,1,0:T(8,128)S(1)}, f32[1,8,256]{2,1,0:T(8,128)S(1)}, f32[1,8,256,128]{3,2,1,0:T(8,128)S(1)}) %tuple.78, (s32[]{:T(128)}, s32[]{:T(128)}, s32[]{:T(128)}, ...), branch_computations={%region_6.6_spmd, %region_7.10_spmd.clone} | conditional | flops 272780096 | bytes 9328974 | solution.py:169
  152.2 4.2 %conditional.2 = ((f32[1,8,256]{2,1,0:T(8,128)S(1)}, f32[1,8,256]{2,1,0:T(8,128)S(1)}, f32[1,8,256,128]{3,2,1,0:T(8,128)S(1)})) conditional(s32[]{:T(128)} %convert_element_type.89, (f32[1,8,256]{2,1,0:T(8,128)S(1)}, f32[1,8,256]{2,1,0:T(8,128)S(1)}, f32[1,8,256,128]{3,2,1,0:T(8,128)S(1)}) %tuple.78, (s32[]{:T(128)}, s32[]{:T(128)}, s32[]{:T(128)}, ...), branch_computations={%region_6.6_spmd, %region_7.10_spmd.clone} | conditional | flops 272780096 | bytes 9328974 | solution.py:169
  157.8 4.2 %conditional.2 = ((f32[1,8,256]{2,1,0:T(8,128)S(1)}, f32[1,8,256]{2,1,0:T(8,128)S(1)}, f32[1,8,256,128]{3,2,1,0:T(8,128)S(1)})) conditional(s32[]{:T(128)} %convert_element_type.89, (f32[1,8,256]{2,1,0:T(8,128)S(1)}, f32[1,8,256]{2,1,0:T(8,128)S(1)}, f32[1,8,256,128]{3,2,1,0:T(8,128)S(1)}) %tuple.78, (s32[]{:T(128)}, s32[]{:T(128)}, s32[]{:T(128)}, ...), branch_computations={%region_6.6_spmd, %region_7.10_spmd.clone} | conditional | flops 272780096 | bytes 9328974 | solution.py:169
  163.4 4.2 %conditional.2 = ((f32[1,8,256]{2,1,0:T(8,128)S(1)}, f32[1,8,256]{2,1,0:T(8,128)S(1)}, f32[1,8,256,128]{3,2,1,0:T(8,128)S(1)})) conditional(s32[]{:T(128)} %convert_element_type.89, (f32[1,8,256]{2,1,0:T(8,128)S(1)}, f32[1,8,256]{2,1,0:T(8,128)S(1)}, f32[1,8,256,128]{3,2,1,0:T(8,128)S(1)}) %tuple.78, (s32[]{:T(128)}, s32[]{:T(128)}, s32[]{:T(128)}, ...), branch_computations={%region_6.6_spmd, %region_7.10_spmd.clone} | conditional | flops 272780096 | bytes 9328974 | solution.py:169
  169.2 3.2 %multiply_reduce_fusion = bf16[8,128,128]{2,1,0:T(8,128)(2,1)S(1)} fusion(bf16[8,16,128,128]{3,2,0,1:T(8,128)(2,1)} %bitcast.110, f32[8,16]{0,1:T(8,128)S(1)} %select_bitcast_fusion), kind=kLoop, calls=%fused_computation.27 | loop fusion | flops 6160384 | bytes 4456960 | tf_op jit(solution)/shard_map/nh,nhde->hde/dot_general | solution.py:117
  (267 shorter events, 76.9 us)
Async XLA Ops:
  7.2 14.3 %copy-start = (bf16[256,1024]{1,0:T(8,128)(2,1)S(1)}, bf16[256,1024]{1,0:T(8,128)(2,1)}, u32[]{:S(2)}) copy-start(bf16[256,1024]{1,0:T(8,128)(2,1)} %param.13) | copy-start | bytes 1572868
  7.2 14.3 %copy-start.5 = (bf16[256,1024]{1,0:T(8,128)(2,1)S(1)}, bf16[256,1024]{1,0:T(8,128)(2,1)}, u32[]{:S(2)}) copy-start(bf16[256,1024]{1,0:T(8,128)(2,1)} %param.15) | copy-start | bytes 1572868
  7.2 68.1 %all-gather.4.cloned.1.call-start = ((), (), s32[]{:S(2)}) async-start(), calls=%async_computation.1 | async-start | bytes 2228224 | tf_op jit(solution)/shard_map/all_gather | solution.py:31
  8.9 160.2 %all-gather.6.cloned.1.call-start = ((), (), s32[]{:S(2)}) async-start(), calls=%async_computation.2 | async-start | bytes 4456448 | tf_op jit(solution)/shard_map/all_gather | solution.py:112
  16.8 14.5 %all-to-all-start = ((f32[16,1,8]{2,1,0:T(1,128)}), f32[16,1,8]{2,1,0:T(1,128)S(1)}, u32[]{:S(2)}, u32[]{:S(2)}) async-start(f32[16,1,8]{2,1,0:T(1,128)} %broadcast_in_dim.173), calls=%async_computation | async-start | bytes 16384 | tf_op jit(solution)/shard_map/all_to_all | solution.py:11
  21.5 2.2 %copy-start.2 = (bf16[256,1024]{1,0:T(8,128)(2,1)S(1)}, bf16[256,1024]{1,0:T(8,128)(2,1)}, u32[]{:S(2)}) copy-start(bf16[256,1024]{1,0:T(8,128)(2,1)} %param.18) | copy-start | bytes 1572868
  31.5 46.6 %copy-start.3 = (s32[16]{0:T(128)S(1)}, s32[16]{0:T(128)}, u32[]{:S(2)}) copy-start(s32[16]{0:T(128)} %param.21) | copy-start | bytes 196
  169.2 3.2 %copy-start.1 = (f32[256,8,128]{0,2,1:T(8,128)S(1)}, f32[256,8,128]{0,2,1:T(8,128)}, u32[]{:S(2)}) copy-start(f32[256,8,128]{0,2,1:T(8,128)} %convolution_bitcast_fusion.2) | copy-start | bytes 3145732
  172.3 0.7 copy-start.4
Sparse Core Ops, SparseCore 0:
  10.4 64.8 all-gather.3
  77.7 73.0 all-gather.5
where the time goes:
time: 184 us; the launch traced here: 181 us
  waiting for transfers between devices  51.1 us (28%)
  matrix products  41.8 us (23%)
  other arithmetic  37.7 us (20%)
  local copies, waits for them, and re-layouts  17.9 us (10%)
  between operations  14.3 us (8%)
  loops' own time  13.7 us (7%)
  starting transfers between devices  4.67 us (3%)
    all_gather x1, waiting for transfers between devices, side_by_side(): lax.all_gather(both, axis, axis=dim, tiled=True)  43.8 us
    dot_general x16, matrix products, attend_keys(): jnp.einsum('tkgd,skd->kgts', query_block, key_block, preferred_element_ty...  20.7 us
    dot_general x16, matrix products, attend_keys(): jnp.einsum('kgts,skd->kgtd', weights_now.astype(jnp.bfloat16), value_bloc...  16.5 us
    reduce_sum x17, other arithmetic, live_slots(): own_length = jnp.sum(jnp.where(owners == device, lengths, 0))  11.9 us
    another operation x1, loops' own time, body(): lax.scan(per_shard, states, (key_stack, value_stack, jnp.arange(shard_cou...  11.9 us
    dynamic_slice x16, local copies, waits for them, and re-layouts, body(): lax.scan(per_shard, states, (key_stack, value_stack, jnp.arange(shard_cou...  10.6 us
    lt x17, other arithmetic, live_slots(): return jnp.arange(row_count, dtype=jnp.int32) < own_length  10.4 us
    all_to_all x1, waiting for transfers between devices, sent_to_all(): lax.all_to_all(jnp.broadcast_to(x[None], (length, *x.shape)), axis, 0, 0,...  7.14 us
  transfers between devices with their start and end apart: 3, of which 2 were waited for; matrix products, arithmetic and copies ran while one was open for 50% of the time, Pallas kernels for 0%

commit v1 on v0

v1 whole, which is shorter than its diff:
```python
import functools
import math

import jax
import jax.numpy as jnp
from jax import lax
from jax.experimental import pallas as pl
from jax.experimental.pallas import tpu as pltpu
from jax.sharding import PartitionSpec as P

MESH = pl.DeviceIdType.MESH
F32 = jnp.float32
BF16 = jnp.bfloat16
MASKED = -1e30
TICKS = 4


def dot(a, b, contract=(1, 0), precision=None):
    return lax.dot_general(
        a,
        b,
        (((contract[0],), (contract[1],)), ((), ())),
        precision=precision,
        preferred_element_type=F32,
    )


def kernel(
    n,
    up_hops,
    lq_ref,
    lk_ref,
    lv_ref,
    decay_ref,
    gain_ref,
    sq_ref,
    sk_ref,
    sv_ref,
    len_ref,
    lo_ref,
    so_ref,
    kbuf,
    vbuf,
    ebuf,
    obuf,
    state,
    inside,
    qt,
    ot,
    peak,
    total,
    cum,
    cum_t,
    keep,
    bias_ref,
    recv_k,
    recv_v,
    send_k,
    send_v,
    chain_recv,
    chain_send,
):
    down_hops = n - 1 - up_hops
    me = lax.axis_index("seq")
    right, left = lax.rem(me + 1, n), lax.rem(me + n - 1, n)
    toks, width = sk_ref.shape
    heads = decay_ref.shape[1]
    score_scale = width ** (-0.5)
    exp2_scale = score_scale * math.log2(math.e)

    barrier = pltpu.get_barrier_semaphore()
    for neighbour in (left, right):
        pl.semaphore_signal(barrier, inc=1, device_id={"seq": neighbour}, device_id_type=MESH)
    pl.semaphore_wait(barrier, 2)

    def block_copies(k_src, v_src, s, direction, hop):
        target = right if direction == 0 else left
        return (
            pltpu.make_async_remote_copy(
                src_ref=k_src,
                dst_ref=kbuf.at[s],
                send_sem=send_k.at[direction, hop],
                recv_sem=recv_k.at[s],
                device_id={"seq": target},
                device_id_type=MESH,
            ),
            pltpu.make_async_remote_copy(
                src_ref=v_src,
                dst_ref=vbuf.at[s],
                send_sem=send_v.at[direction, hop],
                recv_sem=recv_v.at[s],
                device_id={"seq": target},
                device_id_type=MESH,
            ),
        )

    def chain_copy(h):
        return pltpu.make_async_remote_copy(
            src_ref=obuf.at[h],
            dst_ref=ebuf.at[h],
            send_sem=chain_send.at[h],
            recv_sem=chain_recv.at[h],
            device_id={"seq": right},
            device_id_type=MESH,
        )

    @pl.when(me < n - 1)
    def _():
        for copy in block_copies(sk_ref, sv_ref, me, 0, 0):
            copy.start()

    @pl.when(me < down_hops)
    def _():
        for copy in block_copies(sk_ref, sv_ref, me, 1, 0):
            copy.start()

    own_length = len_ref[me]
    row_of = lax.broadcasted_iota(jnp.int32, (toks, toks), 0)
    col_of = lax.broadcasted_iota(jnp.int32, (toks, toks), 1)
    live_col = lax.broadcasted_iota(jnp.int32, (toks, heads), 0) < own_length
    masked = jnp.where(live_col, decay_ref[...], 0.0)
    running = dot((row_of >= col_of).astype(F32), masked, precision=lax.Precision.HIGHEST)
    cum[...] = running
    cum_t[...] = dot(
        masked, (row_of <= col_of).astype(F32), (0, 0), precision=lax.Precision.HIGHEST
    )
    keep[...] = jnp.broadcast_to(jnp.exp(cum_t[:, toks - 1 : toks]), (heads, width))
    fading = jnp.where(live_col, jnp.exp(running[toks - 1 : toks, :] - running), 0.0)
    for h in range(heads):
        cols = slice(h * width, (h + 1) * width)
        block_keys = (lk_ref[:, cols].astype(F32) * fading[:, h : h + 1]).astype(BF16)
        own_state = dot(block_keys, lv_ref[:, cols], (0, 0))
        state[h] = own_state

        @pl.when(me == 0)
        def _():
            obuf[h] = own_state.astype(BF16)
            ebuf[h] = jnp.zeros((width, width), BF16)
            chain_copy(h).start()

    causal = row_of >= col_of
    for h in range(heads):
        cols = slice(h * width, (h + 1) * width)
        scores = dot(lq_ref[:, cols], lk_ref[:, cols], (1, 1))
        gaps = jnp.where(causal, cum[:, h : h + 1] - cum_t[h : h + 1, :], MASKED)
        weights = (scores * score_scale * jnp.exp(gaps)).astype(BF16)
        inside[:, cols] = dot(weights, lv_ref[:, cols])

    def attend_head(h, scores, v_t, first):
        block_peak = jnp.max(scores, axis=0, keepdims=True)
        if first:
            new_peak = block_peak
        else:
            old_peak = peak[pl.ds(h, 1), :]
            new_peak = jnp.maximum(old_peak, block_peak)
        probs = jnp.exp2((scores - new_peak) * exp2_scale)
        block_total = jnp.sum(probs, axis=0, keepdims=True)
        block_out = dot(v_t, probs.astype(BF16))
        peak[pl.ds(h, 1), :] = new_peak
        if first:
            total[pl.ds(h, 1), :] = block_total
            ot[h] = block_out
        else:
            shrink = jnp.exp2((old_peak - new_peak) * exp2_scale)
            total[pl.ds(h, 1), :] = total[pl.ds(h, 1), :] * shrink + block_total
            ot[h] = ot[h] * shrink + block_out

    seen = (row_of <= col_of) & (row_of < own_length)
    own_v_t = sv_ref[...].T
    for h in range(heads):
        q_t = sq_ref[:, h * width : (h + 1) * width].T
        qt[h] = q_t
        scores = jnp.where(seen, dot(sk_ref[...], q_t), MASKED)
        attend_head(h, scores, own_v_t, True)

    half = heads // 2

    def attend_block(s, first_head):
        dead = lax.broadcasted_iota(jnp.int32, (toks, width), 0) >= len_ref[s]
        bias_ref[...] = jnp.where(dead, MASKED, 0.0)
        k_block = kbuf[s]
        v_t = vbuf[s].T
        for i in range(half):
            h = first_head + i
            bias = bias_ref[...]
            scores = dot(k_block, qt[h]) + jnp.concatenate([bias] * (toks // width), axis=1)
            attend_head(h, scores, v_t, False)

    def finish_light(h, entering):
        cols = pl.ds(pl.multiple_of(h * width, width), width)
        pick = (lax.broadcasted_iota(jnp.int32, (toks, heads), 1) == h).astype(F32)
        grown = jnp.exp(jnp.sum(cum[...] * pick, axis=1, keepdims=True)) * score_scale
        combined = inside[:, cols] + dot(lq_ref[:, cols], entering) * grown
        mean = jnp.mean(combined * combined, axis=1, keepdims=True)
        normed = combined * lax.rsqrt(mean + 1e-6) * gain_ref[:, cols]
        alive = lax.broadcasted_iota(jnp.int32, (toks, width), 0) < own_length
        lo_ref[:, cols] = jnp.where(alive, normed, 0.0).astype(BF16)

    def tick(t, carry):
        hop = t // TICKS + 1
        phase = lax.rem(t, TICKS)
        up_block = me - hop
        down_block = lax.rem(me + hop, n)
        has_up = (hop <= up_hops) & (up_block >= 0)
        has_down = (hop <= down_hops) & (down_block < down_hops)

        @pl.when((phase == 0) & has_up)
        def _():
            s = up_block
            copies = block_copies(kbuf.at[s], vbuf.at[s], s, 0, hop)
            for copy in copies:
                copy.wait_recv()

                @pl.when((hop < up_hops) & (me < n - 1))
                def _():
                    copy.start()

        @pl.when((phase == 0) & has_down)
        def _():
            s = down_block
            copies = block_copies(kbuf.at[s], vbuf.at[s], s, 1, hop)
            for copy in copies:
                copy.wait_recv()

                @pl.when(hop < down_hops)
                def _():
                    copy.start()

        h = t - me * TICKS

        @pl.when((h >= 0) & (h < heads))
        def _():
            @pl.when(me > 0)
            def _():
                chain_copy(h).wait_recv()

            entering = ebuf[h]

            @pl.when((me > 0) & (me < n - 1))
            def _():
                obuf[h] = (entering.astype(F32) * keep[pl.ds(h, 1), :] + state[h]).astype(BF16)
                chain_copy(h).start()

            finish_light(h, entering)

        @pl.when((phase < 2) & has_up)
        def _():
            attend_block(up_block, phase * half)

        @pl.when((phase >= 2) & has_down & (down_block < me))
        def _():
            attend_block(down_block, (phase - 2) * half)

        return carry

    lax.fori_loop(0, max((n - 1) * TICKS + heads, max(up_hops, down_hops) * TICKS), tick, 0)

    alive_q = lax.broadcasted_iota(jnp.int32, (1, toks), 1) < own_length
    for h in range(heads):
        norm = jnp.where(alive_q, 1.0 / total[h : h + 1, :], 0.0)
        so_ref[:, h * width : (h + 1) * width] = (ot[h] * norm).T.astype(BF16)

    def drain(hop, carry):
        up_block = me - hop
        down_block = lax.rem(me + hop, n)

        @pl.when((hop < up_hops) & (up_block >= 0) & (me < n - 1))
        def _():
            for copy in block_copies(kbuf.at[up_block], vbuf.at[up_block], up_block, 0, hop):
                copy.wait_send()

        @pl.when((hop < down_hops) & (down_block < down_hops))
        def _():
            for copy in block_copies(kbuf.at[down_block], vbuf.at[down_block], down_block, 1, hop):
                copy.wait_send()

        return carry

    lax.fori_loop(0, max(up_hops, down_hops), drain, 0)

    @pl.when(me < n - 1)
    def _():
        for h in range(heads):
            chain_copy(h).wait_send()


def body(n, *args):
    toks, columns = args[0].shape
    width = args[6].shape[1]
    heads = columns // width
    up_hops = (n - 1) // 2
    hops = n - 1 - up_hops
    vmem = pl.BlockSpec(memory_space=pltpu.VMEM)
    smem = pl.BlockSpec(memory_space=pltpu.SMEM)
    gain = args[4].reshape(1, columns)
    out = jax.ShapeDtypeStruct((toks, columns), BF16)
    return pl.pallas_call(
        functools.partial(kernel, n, up_hops),
        out_shape=(out, out),
        in_specs=[vmem] * 8 + [smem],
        out_specs=(vmem, vmem),
        scratch_shapes=[
            pltpu.VMEM((n, toks, width), BF16),
            pltpu.VMEM((n, toks, width), BF16),
            pltpu.VMEM((heads, width, width), BF16),
            pltpu.VMEM((heads, width, width), BF16),
            pltpu.VMEM((heads, width, width), F32),
            pltpu.VMEM((toks, columns), F32),
            pltpu.VMEM((heads, width, toks), BF16),
            pltpu.VMEM((heads, width, toks), F32),
            pltpu.VMEM((heads, toks), F32),
            pltpu.VMEM((heads, toks), F32),
            pltpu.VMEM((toks, heads), F32),
            pltpu.VMEM((heads, toks), F32),
            pltpu.VMEM((heads, width), F32),
            pltpu.VMEM((toks, width), F32),
            pltpu.SemaphoreType.DMA((n,)),
            pltpu.SemaphoreType.DMA((n,)),
            pltpu.SemaphoreType.DMA((2, hops + 1)),
            pltpu.SemaphoreType.DMA((2, hops + 1)),
            pltpu.SemaphoreType.DMA((heads,)),
            pltpu.SemaphoreType.DMA((heads,)),
        ],
        compiler_params=pltpu.CompilerParams(
            collective_id=0, has_side_effects=True, vmem_limit_bytes=48 * 1024 * 1024
        ),
    )(*args[:4], gain, *args[5:])


def solution(mesh):
    tokens = P(("groups", "seq"), ("section", "mp"))
    return jax.shard_map(
        functools.partial(body, mesh.shape["seq"]),
        mesh=mesh,
        in_specs=(tokens,) * 4 + (P(("section", "mp")),) + (tokens,) * 3 + (P("groups"),),
        out_specs=(tokens, tokens),
        check_vma=False,
    )
```

time: 184 us -> 69.1 us (0.38); the launches traced: 181 us -> 68.7 us
  Pallas kernels: 0 us -> 61.4 us
  waiting for transfers between devices: 51.1 us -> 0 us
  matrix products: 41.8 us -> 0 us
  other arithmetic: 37.7 us -> 0 us
  loops' own time: 13.7 us -> 0 us
  between operations: 14.3 us -> 0.72 us
  local copies, waits for them, and re-layouts: 17.9 us -> 6.64 us
  starting transfers between devices: 4.67 us -> 0 us
    pallas_call x0 -> x1, Pallas kernels: none -> 61.4 us  [body(): pl.pallas_call(functools.partial(kernel, n, up_hops), out_shape=(out, out...]
    all_gather x2 -> x0, waiting for transfers between devices: 43.8 us -> none  [the longest x1 43.8 us: side_by_side(): lax.all_gather(both, axis, axis=dim, tiled=True)]
    dot_general x35 -> x0, matrix products: 41.8 us -> none  [the longest x16 20.7 us: attend_keys(): jnp.einsum('tkgd,skd->kgts', query_block, key_block, preferred_element_ty...]
    reduce_sum x34 -> x0, other arithmetic: 16.7 us -> none  [the longest x17 11.9 us: live_slots(): own_length = jnp.sum(jnp.where(owners == device, lengths, 0))]
    another operation x17 -> x0, loops' own time: 13.7 us -> none  [the longest x1 11.9 us: body(): lax.scan(per_shard, states, (key_stack, value_stack, jnp.arange(shard_cou...]
    dynamic_slice x16 -> x0, local copies, waits for them, and re-layouts: 10.6 us -> none  [body(): lax.scan(per_shard, states, (key_stack, value_stack, jnp.arange(shard_cou...]
    lt x18 -> x0, other arithmetic: 10.4 us -> none  [the longest x17 10.4 us: live_slots(): return jnp.arange(row_count, dtype=jnp.int32) < own_length]
    all_to_all x1 -> x0, waiting for transfers between devices: 7.14 us -> none  [sent_to_all(): lax.all_to_all(jnp.broadcast_to(x[None], (length, *x.shape)), axis, 0, 0,...]
  transfers between devices with their start and end apart: 3 -> 0, of which waited for: 2 -> 0; matrix products, arithmetic and copies ran while one was open for 50% -> 0% of each run, Pallas kernels for 0% -> 0%
where the time goes in v1:
time: 69.1 us; the launch traced here: 68.7 us
  Pallas kernels  61.4 us (89%)
  local copies, waits for them, and re-layouts  6.64 us (10%)
  between operations  0.72 us (1%)
    pallas_call x1, Pallas kernels, body(): pl.pallas_call(functools.partial(kernel, n, up_hops), out_shape=(out, out...  61.4 us
    unnamed x19, local copies, waits for them, and re-layouts  6.64 us

profile of v1, /device:TPU:1952, one launch (start us, length us, event | category | flops | bytes accessed | tf_op | source)
XLA Modules:
  0.0 68.7 jit_solution(5865569928940927174)
XLA Ops:
  0.6 0.0 copy-start.4
  0.6 0.0 copy-start.5
  0.7 0.0 copy-start.6
  0.7 0.0 copy-start.7
  0.7 0.9 %copy.11.decay_ref = f32[256,8]{1,0:T(8,128)S(1)} copy(f32[256,8]{0,1:T(8,128)} %param.12) | data formatting | bytes 16384 | tf_op args[3]
  1.6 0.0 copy-done.4
  1.6 0.0 copy-done.5
  1.6 0.0 copy-done.6
  1.6 0.0 copy-done.7
  1.6 0.0 copy-start
  1.6 1.0 %copy-done = bf16[256,1024]{1,0:T(8,128)(2,1)S(1)} copy-done((bf16[256,1024]{1,0:T(8,128)(2,1)S(1)}, bf16[256,1024]{1,0:T(8,128)(2,1)}, u32[]{:S(2)}) %copy-start) | copy-done | bytes 524312
  2.6 0.0 copy-start.1
  2.6 1.0 %copy-done.1 = bf16[256,1024]{1,0:T(8,128)(2,1)S(1)} copy-done((bf16[256,1024]{1,0:T(8,128)(2,1)S(1)}, bf16[256,1024]{1,0:T(8,128)(2,1)}, u32[]{:S(2)}) %copy-start.1) | copy-done | bytes 524312
  3.7 0.0 copy-start.2
  3.7 1.0 %copy-done.2 = bf16[256,1024]{1,0:T(8,128)(2,1)S(1)} copy-done((bf16[256,1024]{1,0:T(8,128)(2,1)S(1)}, bf16[256,1024]{1,0:T(8,128)(2,1)}, u32[]{:S(2)}) %copy-start.2) | copy-done | bytes 524312
  4.7 0.0 copy-start.3
  4.7 1.0 %copy-done.3 = bf16[256,1024]{1,0:T(8,128)(2,1)S(1)} copy-done((bf16[256,1024]{1,0:T(8,128)(2,1)S(1)}, bf16[256,1024]{1,0:T(8,128)(2,1)}, u32[]{:S(2)}) %copy-start.3) | copy-done | bytes 524312
  5.8 61.4 %shard_map.104 = (bf16[256,1024]{1,0:T(8,128)(2,1)S(1)}, bf16[256,1024]{1,0:T(8,128)(2,1)S(1)}) custom-call(bf16[256,1024]{1,0:T(8,128)(2,1)S(1)} %copy-done, bf16[256,1024]{1,0:T(8,128)(2,1)S(1)} %copy-done.1, bf16[256,1024]{1,0:T(8,128)(2,1)S(1)} %copy-done.2, f32[256,8]{1,0:T(8,128)S(1)} %copy.11.decay_ref, f32[1,1024]{1,0:T(1,128)S(1)} %bitcast.1, ...), custom_call_target="tpu_custom_call" | custom-call | tf_op jit(solution)/shard_map/pallas_call | solution.py:297
  67.2 0.8 %copy.14 = bf16[256,1024]{1,0:T(8,128)(2,1)} copy(bf16[256,1024]{1,0:T(8,128)(2,1)S(1)} %get-tuple-element.4) | data formatting | bytes 1048576
  68.0 0.8 %copy.15 = bf16[256,1024]{1,0:T(8,128)(2,1)} copy(bf16[256,1024]{1,0:T(8,128)(2,1)S(1)} %get-tuple-element.5) | data formatting | bytes 1048576
Async XLA Ops:
  0.6 0.9 %copy-start.4 = (bf16[256,128]{1,0:T(8,128)(2,1)S(1)}, bf16[256,128]{1,0:T(8,128)(2,1)}, u32[]{:S(2)}) copy-start(bf16[256,128]{1,0:T(8,128)(2,1)} %sk_ref.1) | copy-start | bytes 196612
  0.6 0.9 %copy-start.5 = (bf16[256,128]{1,0:T(8,128)(2,1)S(1)}, bf16[256,128]{1,0:T(8,128)(2,1)}, u32[]{:S(2)}) copy-start(bf16[256,128]{1,0:T(8,128)(2,1)} %sv_ref.1) | copy-start | bytes 196612
  0.7 0.9 %copy-start.6 = (f32[1024]{0:T(1024)S(1)}, f32[1024]{0:T(1024)}, u32[]{:S(2)}) copy-start(f32[1024]{0:T(1024)} %param.13) | copy-start | bytes 12292
  0.7 0.9 %copy-start.7 = (s32[16]{0:T(128)S(1)}, s32[16]{0:T(128)}, u32[]{:S(2)}) copy-start(s32[16]{0:T(128)} %len_ref.1) | copy-start | bytes 196
  1.6 1.0 %copy-start = (bf16[256,1024]{1,0:T(8,128)(2,1)S(1)}, bf16[256,1024]{1,0:T(8,128)(2,1)}, u32[]{:S(2)}) copy-start(bf16[256,1024]{1,0:T(8,128)(2,1)} %lq_ref.1) | copy-start | bytes 1572868
  2.6 1.0 %copy-start.1 = (bf16[256,1024]{1,0:T(8,128)(2,1)S(1)}, bf16[256,1024]{1,0:T(8,128)(2,1)}, u32[]{:S(2)}) copy-start(bf16[256,1024]{1,0:T(8,128)(2,1)} %lk_ref.1) | copy-start | bytes 1572868
  3.7 1.0 %copy-start.2 = (bf16[256,1024]{1,0:T(8,128)(2,1)S(1)}, bf16[256,1024]{1,0:T(8,128)(2,1)}, u32[]{:S(2)}) copy-start(bf16[256,1024]{1,0:T(8,128)(2,1)} %lv_ref.1) | copy-start | bytes 1572868
  4.7 1.0 %copy-start.3 = (bf16[256,1024]{1,0:T(8,128)(2,1)S(1)}, bf16[256,1024]{1,0:T(8,128)(2,1)}, u32[]{:S(2)}) copy-start(bf16[256,1024]{1,0:T(8,128)(2,1)} %sq_ref.1) | copy-start | bytes 1572868

commit v2 on v1

v2 whole, which is shorter than its diff:
```python
import functools
import math

import jax
import jax.numpy as jnp
from jax import lax
from jax.experimental import pallas as pl
from jax.experimental.pallas import tpu as pltpu
from jax.sharding import PartitionSpec as P

MESH = pl.DeviceIdType.MESH
F32 = jnp.float32
BF16 = jnp.bfloat16
MASKED = -1e30
HOP_TICKS = 5
FIRST_TICK = 0
WRAP_STEP = 3
UP_EXTRA = 1


def dot(a, b, contract=(1, 0), precision=None):
    return lax.dot_general(
        a,
        b,
        (((contract[0],), (contract[1],)), ((), ())),
        precision=precision,
        preferred_element_type=F32,
    )


def kernel(
    n,
    up_hops,
    lq_hbm,
    lk_hbm,
    lv_hbm,
    decay_ref,
    gain_ref,
    sq_hbm,
    sk_hbm,
    sv_hbm,
    len_ref,
    lo_ref,
    so_ref,
    lq_ref,
    lk_ref,
    lv_ref,
    sq_ref,
    kbuf,
    vbuf,
    ebuf,
    obuf,
    state,
    inside,
    qt,
    ot,
    peak,
    total,
    cum,
    cum_t,
    keep,
    bias_ref,
    vt_ref,
    ready_sem,
    load_sem,
    recv_k,
    recv_v,
    send_k,
    send_v,
    chain_recv,
    chain_send,
):
    down_hops = n - 1 - up_hops
    me = lax.axis_index("seq")
    last = n - 1
    right = jnp.minimum(me + 1, last)
    left = jnp.where(me == 0, last, me - 1)
    toks, width = sk_hbm.shape
    heads = decay_ref.shape[0]
    score_scale = width ** (-0.5)
    exp2_scale = score_scale * math.log2(math.e)

    loads = {}
    for i, (name, src, dst) in enumerate(
        (
            ("sk", sk_hbm, kbuf.at[me]),
            ("sv", sv_hbm, vbuf.at[me]),
            ("lk", lk_hbm, lk_ref),
            ("lv", lv_hbm, lv_ref),
            ("lq", lq_hbm, lq_ref),
            ("sq", sq_hbm, sq_ref),
        )
    ):
        loads[name] = pltpu.make_async_copy(src, dst, load_sem.at[i])
        loads[name].start()

    barrier = pltpu.get_barrier_semaphore()

    def tell(semaphore, device):
        pl.semaphore_signal(semaphore, inc=1, device_id={"seq": device}, device_id_type=MESH)

    @pl.when(me > 0)
    def _():
        tell(barrier, me - 1)

    @pl.when(me < last)
    def _():
        tell(barrier, me + 1)

    @pl.when(me == 0)
    def _():
        tell(barrier, last)

    @pl.when(me == 0)
    def _():
        pl.semaphore_wait(barrier, 1)

    @pl.when(me > 0)
    def _():
        pl.semaphore_wait(barrier, 2)

    @pl.when(me == last)
    def _():
        tell(ready_sem, 0)

    def block_copies(s, direction):
        target = right if direction == 0 else left
        return (
            pltpu.make_async_remote_copy(
                src_ref=kbuf.at[s],
                dst_ref=kbuf.at[s],
                send_sem=send_k.at[direction, s],
                recv_sem=recv_k.at[s],
                device_id={"seq": target},
                device_id_type=MESH,
            ),
            pltpu.make_async_remote_copy(
                src_ref=vbuf.at[s],
                dst_ref=vbuf.at[s],
                send_sem=send_v.at[direction, s],
                recv_sem=recv_v.at[s],
                device_id={"seq": target},
                device_id_type=MESH,
            ),
        )

    def chain_copy(h):
        return pltpu.make_async_remote_copy(
            src_ref=obuf.at[h],
            dst_ref=ebuf.at[h],
            send_sem=chain_send.at[h],
            recv_sem=chain_recv.at[h],
            device_id={"seq": right},
            device_id_type=MESH,
        )

    loads["sk"].wait()
    loads["sv"].wait()

    @pl.when(me < last)
    def _():
        for copy in block_copies(me, 0):
            copy.start()

    @pl.when((me > 0) & (me < down_hops))
    def _():
        for copy in block_copies(me, 1):
            copy.start()

    own_length = len_ref[me]
    row_of = lax.broadcasted_iota(jnp.int32, (toks, toks), 0)
    col_of = lax.broadcasted_iota(jnp.int32, (toks, toks), 1)
    until = (row_of <= col_of).astype(F32).astype(BF16)
    live_row = lax.broadcasted_iota(jnp.int32, (heads, toks), 1) < own_length
    masked = jnp.where(live_row, decay_ref[...], 0.0)
    high = masked.astype(BF16).astype(F32)
    middle = (masked - high).astype(BF16).astype(F32)
    low = masked - high - middle
    sums = dot(jnp.concatenate([high, middle, low], axis=0).astype(BF16), until)
    running_t = sums[:heads] + sums[heads : 2 * heads] + sums[2 * heads :]
    cum_t[...] = running_t
    keep[...] = jnp.broadcast_to(jnp.exp(running_t[:, toks - 1 :]), (heads, width))
    cum[...] = running_t.T
    faded_t = jnp.where(live_row, jnp.exp(running_t[:, toks - 1 :] - running_t), 0.0)
    fading = faded_t.T

    loads["lk"].wait()
    loads["lv"].wait()
    for h in range(heads):
        cols = slice(h * width, (h + 1) * width)
        block_keys = (lk_ref[:, cols].astype(F32) * fading[:, h : h + 1]).astype(BF16)
        state[h] = dot(block_keys, lv_ref[:, cols], (0, 0))

    @pl.when(me == 0)
    def _():
        for h in range(heads):
            obuf[h] = state[h].astype(BF16)
            ebuf[h] = jnp.zeros((width, width), BF16)
        for h in range(heads):
            chain_copy(h).start()

    loads["lq"].wait()
    causal = row_of >= col_of

    def light_scores(h):
        cols = slice(h * width, (h + 1) * width)
        return dot(lq_ref[:, cols], lk_ref[:, cols], (1, 1))

    ahead = [light_scores(0), light_scores(1)]
    for h in range(heads):
        cols = slice(h * width, (h + 1) * width)
        gaps = jnp.where(causal, cum[:, h : h + 1] - cum_t[h : h + 1, :], MASKED)
        weights = (ahead[h] * score_scale * jnp.exp(gaps)).astype(BF16)
        if h + 2 < heads:
            ahead.append(light_scores(h + 2))
        inside[:, cols] = dot(weights, lv_ref[:, cols])

    def attend(hs, scores_of, values_t, first):
        ahead = [scores_of(h) for h in hs[:2]]
        for i, h in enumerate(hs):
            scores = ahead[i]
            row = slice(h, h + 1)
            new_peak = jnp.max(scores, axis=0, keepdims=True)
            if not first:
                old_peak = peak[row, :]
                new_peak = jnp.maximum(old_peak, new_peak)
            probs = jnp.exp2((scores - new_peak) * exp2_scale)
            block_total = jnp.sum(probs, axis=0, keepdims=True)
            if i + 2 < len(hs):
                ahead.append(scores_of(hs[i + 2]))
            block_out = dot(values_t, probs.astype(BF16))
            peak[row, :] = new_peak
            if first:
                total[row, :] = block_total
                ot[h] = block_out
            else:
                shrink = jnp.exp2((old_peak - new_peak) * exp2_scale)
                total[row, :] = total[row, :] * shrink + block_total
                ot[h] = ot[h] * shrink + block_out

    loads["sq"].wait()
    seen = (row_of <= col_of) & (row_of < own_length)
    own_keys = kbuf[me]
    for h in range(heads):
        qt[h] = sq_ref[:, h * width : (h + 1) * width].T
    attend(
        tuple(range(heads)),
        lambda h: jnp.where(seen, dot(own_keys, qt[h]), MASKED),
        vbuf[me].T,
        True,
    )

    halves = (tuple(range(heads // 2)), tuple(range(heads // 2, heads)))
    per_tick = 2
    events = heads // per_tick

    def finish_light(h, entering):
        cols = slice(h * width, (h + 1) * width)
        grown = jnp.exp(cum[:, h : h + 1]) * score_scale
        combined = inside[:, cols] + dot(lq_ref[:, cols], entering) * grown
        mean = jnp.mean(combined * combined, axis=1, keepdims=True)
        normed = combined * lax.rsqrt(mean + 1e-6) * gain_ref[:, cols]
        alive = lax.broadcasted_iota(jnp.int32, (toks, width), 0) < own_length
        lo_ref[:, cols] = jnp.where(alive, normed, 0.0).astype(BF16)

    def first_tick(device):
        return (device * HOP_TICKS) // 4 + FIRST_TICK

    def chain_events(t):
        for j in range(events):

            @pl.when(t - first_tick(me) == j)
            def _():
                hs = range(j * per_tick, (j + 1) * per_tick)
                for h in hs:

                    @pl.when(me > 0)
                    def _():
                        chain_copy(h).wait_recv()

                    @pl.when((me > 0) & (me < last))
                    def _():
                        obuf[h] = (ebuf[h].astype(F32) * keep[h : h + 1, :] + state[h]).astype(BF16)
                        chain_copy(h).start()

                for h in hs:
                    finish_light(h, ebuf[h])

    def finish_soft():
        alive_q = lax.broadcasted_iota(jnp.int32, (1, toks), 1) < own_length
        for h in range(heads):
            norm = jnp.where(alive_q, 1.0 / total[h : h + 1, :], 0.0)
            so_ref[:, h * width : (h + 1) * width] = (ot[h] * norm).astype(BF16).T

    def plan(hop):
        up_block = me - hop
        has_up = (hop >= 1) & (hop <= up_hops) & (up_block >= 0)
        before = me < down_hops
        down_hop = hop - jnp.where(me == 0, WRAP_STEP, 0)
        down_block = jnp.where(before, me + down_hop, me + down_hop - n)
        arrives = before | (down_hop <= down_hops)
        has_down = (down_hop > 0) & arrives & (down_block >= 0) & (down_block < down_hops)
        return up_block, has_up, before, down_hop, down_block, has_down, has_down & (me >= down_hops)

    def pass_on(hop, part):
        up_block, has_up, before, down_hop, down_block, has_down, _ = plan(hop)

        @pl.when(has_up)
        def _():
            copy = block_copies(up_block, 0)[part]
            copy.wait_recv()

            @pl.when((hop < up_hops) & (me < last))
            def _():
                copy.start()

        @pl.when(has_down)
        def _():
            copy = block_copies(down_block, 1)[part]
            copy.wait_recv()

            @pl.when(before | (down_hop < down_hops))
            def _():
                copy.start()

    def attend_half(hop, half):
        up_block, has_up, _, _, down_block, _, use_down = plan(hop)

        @pl.when(has_up | use_down)
        def _():
            blocks = (jnp.where(has_up, up_block, me), jnp.where(use_down, down_block, me))
            if half == 0:
                used = (has_up, use_down)
                rows = lax.broadcasted_iota(jnp.int32, (toks, width), 0)
                for i in range(2):
                    length = jnp.where(used[i], len_ref[blocks[i]], 0)
                    span = slice(i * toks, (i + 1) * toks)
                    bias_ref[span, :] = jnp.where(rows < length, 0.0, MASKED)
                    vt_ref[:, span] = vbuf[blocks[i]].T
            keys = jnp.concatenate([kbuf[s] for s in blocks], axis=0)

            def scores_of(h):
                bias = bias_ref[...]
                return dot(keys, qt[h]) + jnp.concatenate([bias] * (toks // width), axis=1)

            attend(halves[half], scores_of, vt_ref[...], False)

    def step(hop, carry):
        @pl.when((me == 0) & (hop == WRAP_STEP))
        def _():
            pl.semaphore_wait(ready_sem, 1)
            for copy in block_copies(me, 1):
                copy.start()

        pass_on(hop, 0)
        chain_events(2 * hop - 2)
        attend_half(hop - 1, 1)
        pass_on(hop, 1)

        @pl.when(hop == max(up_hops, down_hops) + 1)
        def _():
            finish_soft()

        chain_events(2 * hop - 1)
        attend_half(hop, 0)
        return carry

    steps = max(
        up_hops + 1,
        down_hops + 1 + WRAP_STEP,
        (first_tick(last) + events + 1) // 2,
    )
    lax.fori_loop(1, steps + 1, step, 0)

    def drain(s, carry):
        @pl.when((s <= me) & (me - s < up_hops) & (me < last))
        def _():
            for copy in block_copies(s, 0):
                copy.wait_send()

        passed = me <= s
        wrapped = me > s + up_hops + 1

        @pl.when((s < down_hops) & (passed | wrapped))
        def _():
            for copy in block_copies(s, 1):
                copy.wait_send()

        return carry

    lax.fori_loop(0, n, drain, 0)

    @pl.when(me < last)
    def _():
        for h in range(heads):
            chain_copy(h).wait_send()


def body(n, *args):
    toks, columns = args[0].shape
    width = args[6].shape[1]
    heads = columns // width
    up_hops = n // 2 + UP_EXTRA
    vmem = pl.BlockSpec(memory_space=pltpu.VMEM)
    hbm = pl.BlockSpec(memory_space=pltpu.HBM)
    smem = pl.BlockSpec(memory_space=pltpu.SMEM)
    gain = args[4].reshape(1, columns)
    out = jax.ShapeDtypeStruct((toks, columns), BF16)
    return pl.pallas_call(
        functools.partial(kernel, n, up_hops),
        out_shape=(out, out),
        in_specs=[hbm] * 3 + [vmem] * 2 + [hbm] * 3 + [smem],
        out_specs=(vmem, vmem),
        scratch_shapes=[
            pltpu.VMEM((toks, columns), BF16),
            pltpu.VMEM((toks, columns), BF16),
            pltpu.VMEM((toks, columns), BF16),
            pltpu.VMEM((toks, columns), BF16),
            pltpu.VMEM((n, toks, width), BF16),
            pltpu.VMEM((n, toks, width), BF16),
            pltpu.VMEM((heads, width, width), BF16),
            pltpu.VMEM((heads, width, width), BF16),
            pltpu.VMEM((heads, width, width), F32),
            pltpu.VMEM((toks, columns), F32),
            pltpu.VMEM((heads, width, toks), BF16),
            pltpu.VMEM((heads, width, toks), F32),
            pltpu.VMEM((heads, toks), F32),
            pltpu.VMEM((heads, toks), F32),
            pltpu.VMEM((toks, heads), F32),
            pltpu.VMEM((heads, toks), F32),
            pltpu.VMEM((heads, width), F32),
            pltpu.VMEM((2 * toks, width), F32),
            pltpu.VMEM((width, 2 * toks), BF16),
            pltpu.SemaphoreType.REGULAR,
            pltpu.SemaphoreType.DMA((6,)),
            pltpu.SemaphoreType.DMA((n,)),
            pltpu.SemaphoreType.DMA((n,)),
            pltpu.SemaphoreType.DMA((2, n)),
            pltpu.SemaphoreType.DMA((2, n)),
            pltpu.SemaphoreType.DMA((heads,)),
            pltpu.SemaphoreType.DMA((heads,)),
        ],
        compiler_params=pltpu.CompilerParams(
            collective_id=0, has_side_effects=True, vmem_limit_bytes=67_043_328
        ),
    )(*args[:3], args[3].T, gain, *args[5:])


def solution(mesh):
    tokens = P(("groups", "seq"), ("section", "mp"))
    return jax.shard_map(
        functools.partial(body, mesh.shape["seq"]),
        mesh=mesh,
        in_specs=(tokens,) * 4 + (P(("section", "mp")),) + (tokens,) * 3 + (P("groups"),),
        out_specs=(tokens, tokens),
        check_vma=False,
    )
```

time: 69.1 us -> 62.4 us (0.903)
  local copies, waits for them, and re-layouts: 6.64 us -> 2.72 us
  Pallas kernels: 61.4 us -> 58.8 us
    unnamed x19 -> x4, local copies, waits for them, and re-layouts: 6.64 us -> 2.72 us
    pallas_call x1, Pallas kernels: 61.4 us -> 58.8 us  [body(): pl.pallas_call(functools.partial(kernel, n, up_hops), out_shape=(out, out...]
where the time goes in v2:
time: 62.4 us; the launch traced here: 62.2 us
  Pallas kernels  58.8 us (94%)
  local copies, waits for them, and re-layouts  2.72 us (4%)
  between operations  0.65 us (1%)
    pallas_call x1, Pallas kernels, body(): pl.pallas_call(functools.partial(kernel, n, up_hops), out_shape=(out, out...  58.8 us
    unnamed x4, local copies, waits for them, and re-layouts  2.72 us

profile of v2, /device:TPU:1952, one launch (start us, length us, event | category | flops | bytes accessed | tf_op | source)
XLA Modules:
  0.0 62.2 jit_solution(1658338584046277423)
XLA Ops:
  0.6 58.8 %shard_map.104 = (bf16[256,1024]{1,0:T(8,128)(2,1)}, bf16[256,1024]{1,0:T(8,128)(2,1)}) custom-call(bf16[256,1024]{1,0:T(8,128)(2,1)} %lq_hbm.1, bf16[256,1024]{1,0:T(8,128)(2,1)} %lk_hbm.1, bf16[256,1024]{1,0:T(8,128)(2,1)} %lv_hbm.1, f32[8,256]{1,0:T(8,128)} %bitcast.2, f32[1,1024]{1,0:T(1,128)} %bitcast.3, bf16[256,1024]{1,0:T(8,128)(2,1)} %sq_hbm.1, ...), custom_call_target="tpu_custom_call" | custom-call | tf_op jit(solution)/shard_map/pallas_call | solution.py:409
  59.4 0.0 copy-start
  59.5 1.9 %copy.13 = bf16[256,1024]{1,0:T(8,128)(2,1)} copy(bf16[256,1024]{1,0:T(8,128)(2,1)} %get-tuple-element.4) | data formatting | bytes 1048576
  61.4 0.0 copy-done
  61.4 0.8 %copy.14 = bf16[256,1024]{1,0:T(8,128)(2,1)} copy(bf16[256,1024]{1,0:T(8,128)(2,1)S(1)} %copy-done) | data formatting | bytes 1048576
Async XLA Ops:
  59.4 1.9 %copy-start = (bf16[256,1024]{1,0:T(8,128)(2,1)S(1)}, bf16[256,1024]{1,0:T(8,128)(2,1)}, u32[]{:S(2)}) copy-start(bf16[256,1024]{1,0:T(8,128)(2,1)} %get-tuple-element.5) | copy-start | bytes 1572868

commit v3 on v2

--- a/solution.py
+++ b/solution.py
@@ -251,7 +251,7 @@
     )
 
     halves = (tuple(range(heads // 2)), tuple(range(heads // 2, heads)))
-    per_tick = 2
+    per_tick = 4
     events = heads // per_tick
 
     def finish_light(h, entering):

time: 62.4 us -> 59 us (0.946)
  Pallas kernels: 58.8 us -> 55.4 us
    pallas_call x1, Pallas kernels: 58.8 us -> 55.4 us  [body(): pl.pallas_call(functools.partial(kernel, n, up_hops), out_shape=(out, out...]
where the time goes in v3:
time: 59 us; the launch traced here: 58.8 us
  Pallas kernels  55.4 us (94%)
  local copies, waits for them, and re-layouts  2.72 us (5%)
  between operations  0.65 us (1%)
    pallas_call x1, Pallas kernels, body(): pl.pallas_call(functools.partial(kernel, n, up_hops), out_shape=(out, out...  55.4 us
    unnamed x4, local copies, waits for them, and re-layouts  2.72 us

profile of v3, /device:TPU:1952, one launch (start us, length us, event | category | flops | bytes accessed | tf_op | source)
XLA Modules:
  0.0 58.8 jit_solution(1582412056583740162)
XLA Ops:
  0.6 55.4 %shard_map.104 = (bf16[256,1024]{1,0:T(8,128)(2,1)}, bf16[256,1024]{1,0:T(8,128)(2,1)}) custom-call(bf16[256,1024]{1,0:T(8,128)(2,1)} %lq_hbm.1, bf16[256,1024]{1,0:T(8,128)(2,1)} %lk_hbm.1, bf16[256,1024]{1,0:T(8,128)(2,1)} %lv_hbm.1, f32[8,256]{1,0:T(8,128)} %bitcast.2, f32[1,1024]{1,0:T(1,128)} %bitcast.3, bf16[256,1024]{1,0:T(8,128)(2,1)} %sq_hbm.1, ...), custom_call_target="tpu_custom_call" | custom-call | tf_op jit(solution)/shard_map/pallas_call | solution.py:409
  56.0 0.0 copy-start
  56.1 1.9 %copy.13 = bf16[256,1024]{1,0:T(8,128)(2,1)} copy(bf16[256,1024]{1,0:T(8,128)(2,1)} %get-tuple-element.4) | data formatting | bytes 1048576
  58.0 0.0 copy-done
  58.0 0.8 %copy.14 = bf16[256,1024]{1,0:T(8,128)(2,1)} copy(bf16[256,1024]{1,0:T(8,128)(2,1)S(1)} %copy-done) | data formatting | bytes 1048576
Async XLA Ops:
  56.0 1.9 %copy-start = (bf16[256,1024]{1,0:T(8,128)(2,1)S(1)}, bf16[256,1024]{1,0:T(8,128)(2,1)}, u32[]{:S(2)}) copy-start(bf16[256,1024]{1,0:T(8,128)(2,1)} %get-tuple-element.5) | copy-start | bytes 1572868
